TPU v7x, 32 devices: a whole 2x2x4 slice. The times are simulated.
32 devices in a mesh: dp: 1, sp: 32 (over x, y, z, core).
Axes of the slice: x: 2, y: 2, z: 4, core: 2. Of those that a mesh axis runs over, the one named last changes fastest.
Arguments:
- q: bfloat16 [32, 56, 128], P('dp')
- k: bfloat16 [32, 4096, 56, 128], P('dp', 'sp')
- v: bfloat16 [32, 4096, 56, 128], P('dp', 'sp')
Outputs:
- q: bfloat16 [32, 56, 128], P('dp')
All inputs are finite; a program needn't handle non-finite values.
Results may differ from a plain program's by a relative error of at most 0.012.
Values are sent between devices in bfloat16 or wider.
A program may use at most 2 GiB of HBM per device.

v0:
```python
import jax
import jax.numpy as jnp
from jax import lax
from jax.sharding import PartitionSpec as P


def einsum(form, a, b):
    return jnp.einsum(form, a.astype(jnp.float32), b.astype(jnp.float32))


def part_of(q, k, v):
    grouped = q.reshape(q.shape[0], k.shape[2], -1, q.shape[2])
    scores = einsum("bgsd,bugd->bgsu", grouped, k) * q.shape[2] ** -0.5
    high = jnp.max(scores, -1, keepdims=True)
    weights = jnp.exp(scores - high)
    seen = einsum("bgsu,bugd->bgsd", weights.astype(jnp.bfloat16), v)
    return jnp.concatenate([seen, jnp.sum(weights, -1, keepdims=True), high], -1)


def together(parts):
    seen, total, high = parts[..., :-2], parts[..., -2:-1], parts[..., -1:]
    scale = jnp.exp(high - jnp.max(high, 0))
    return (jnp.sum(seen * scale, 0) / jnp.sum(total * scale, 0)).astype(jnp.bfloat16)


def solution(mesh):
    def step(q, k, v):
        return together(lax.all_gather(part_of(q, k, v), "sp")).reshape(q.shape)

    return jax.shard_map(
        step,
        mesh=mesh,
        in_specs=(P("dp", None, None), P("dp", "sp", None, None), P("dp", "sp", None, None)),
        out_specs=P("dp", None, None),
        check_vma=False,
    )
```

profile of v0, /device:TPU:0, one launch (start us, length us, event | category | flops | bytes accessed | tf_op | source)
XLA Modules:
  0.0 478.1 jit_solution(18079495155704258004)
XLA Ops:
  6.5 0.0 all-gather.3.cloned.1.call-start
  6.5 38.3 %fusion.3 = f32[32,56,1,128]{3,2,1,0:T(1,128)S(1)} fusion(bf16[32,128,56,128]{3,2,1,0:T(8,128)(2,1)} %param.4, bf16[32,56,128,1]{2,1,0,3:T(8,128)(2,1)} %bitcast.15), kind=kOutput, calls=%fused_computation.4 | convolution fusion | flops 58720256 | bytes 60096512 | tf_op jit(solution)/shard_map/bgsd,bugd->bgsu/dot_general | solution.py:8
  44.8 0.3 multiply_reduce_fusion
  45.2 0.6 fusion.10
  45.8 22.6 %fusion.1 = f32[32,56,1,128]{3,2,1,0:T(1,128)S(1)} fusion(bf16[32,128,56,128]{3,2,1,0:T(8,128)(2,1)} %param.5, bf16[32,56,128,1]{2,1,0,3:T(8,128)(2,1)S(1)} %get-tuple-element.7), kind=kOutput, calls=%fused_computation.2 | convolution fusion | flops 58720256 | bytes 60096512 | tf_op jit(solution)/shard_map/bgsu,bugd->bgsd/dot_general | solution.py:8
  68.4 1.2 copy.12
  69.6 1.6 pad_maximum_fusion
  71.2 0.0 all-gather.3.cloned.1.call-update
  71.2 373.9 %all-gather.3.cloned.1.call-done = f32[1024,56,1,130]{1,0,3,2:T(8,128)} async-done(((f32[32,56,1,130]{1,0,3,2:T(8,128)}), f32[1024,56,1,130]{1,0,3,2:T(8,128)}) %all-gather.3.cloned.1.call-update) | async-done | bytes 29818896 | tf_op jit(solution)/shard_map/all_gather | solution.py:28
  445.2 1.1 slice_reduce_fusion
  446.3 1.3 fusion.9
  447.6 21.6 %fusion = f32[32,56,128]{1,0,2:T(8,128)S(1)} fusion(f32[32,32,56,1,130]{2,1,0,4,3:T(8,128)} %bitcast.7, f32[32,32,56]{2,1,0:T(8,128)S(1)} %get-tuple-element.6), kind=kLoop, calls=%fused_computation.1 | loop fusion | flops 14450688 | bytes 30507008 | tf_op jit(solution)/shard_map/reduce_sum | solution.py:23
  469.2 0.2 divide_convert_fusion
  469.4 1.8 copy.6
Async XLA Ops:
  6.5 438.7 %all-gather.3.cloned.1.call-start = ((), (), s32[]{:S(2)}) async-start(), calls=%async_computation | async-start | bytes 70287360 | tf_op jit(solution)/shard_map/all_gather | solution.py:28
Sparse Core Ops, SparseCore 0:
  71.4 373.7 all-gather.2
where the time goes:
time: 478 us
  waiting for transfers between devices  374 us (78%)
  matrix products  60.9 us (13%)
  other arithmetic  26.8 us (6%)
  between operations  13.4 us (3%)
    all_gather x1, waiting for transfers between devices, step(): return together(lax.all_gather(part_of(q, k, v), 'sp')).reshape(q.shape)  374 us
    dot_general x2, matrix products, einsum(): return jnp.einsum(form, a.astype(jnp.float32), b.astype(jnp.float32))  60.9 us
    reduce_sum x1, other arithmetic, together(): jnp.sum(seen * scale, 0) / jnp.sum(total * scale, 0)  21.6 us
  transfers between devices with their start and end apart: 1, of which 1 were waited for; matrix products, arithmetic and copies ran while one was open for 0% of the time, Pallas kernels for 0%

commit v1 on v0

v1 whole, which is shorter than its diff:
```python
import functools

import jax
import jax.numpy as jnp
from jax import lax
from jax.experimental import pallas as pl
from jax.experimental.pallas import tpu as pltpu
from jax.sharding import PartitionSpec as P

N = 32
S = 32
H = 56
D = 128
G = 7
PAIRS = 64
SLOTS = 4
TAIL = 4
WHOLE = S - TAIL
UNITS = TAIL * G
LAG = 8
SCALE = D**-0.5 * 1.4426950408889634
F32 = jnp.float32
BF16 = jnp.bfloat16


def attend(q, kbuf, vbuf):
    qf = q.astype(F32)
    q2 = jnp.concatenate([qf, qf], 0).astype(BF16)
    col = lax.broadcasted_iota(jnp.int32, (16, 16 * PAIRS), 1)
    row = lax.broadcasted_iota(jnp.int32, (16, 16 * PAIRS), 0)
    mask = (col & 15) == row
    s, m = [], []
    for g in range(G):
        kg = kbuf[:, g].reshape(16 * PAIRS, D)
        x = lax.dot_general(q2[16 * g : 16 * g + 16], kg, (((1,), (1,)), ((), ())), preferred_element_type=F32)
        x = jnp.where(mask, x * SCALE, -jnp.inf)
        s.append(x)
        m.append(jnp.max(x, 1, keepdims=True))
    m = jnp.concatenate(m, 0)
    high = jnp.maximum(m[:H], m[H:])
    both = jnp.concatenate([high, high], 0)
    o, l = [], []
    for g in range(G):
        e = jnp.exp2(s[g] - both[16 * g : 16 * g + 16])
        l.append(jnp.sum(e, 1, keepdims=True))
        o.append(jnp.dot(e.astype(BF16), vbuf[:, g].reshape(16 * PAIRS, D), preferred_element_type=F32))
    l = jnp.concatenate(l, 0)
    o = jnp.concatenate(o, 0)
    return o[:H] + o[H:], high, l[:H] + l[H:]


def kernel(
    q_ref, k_hbm, v_hbm, out, kb, vb, snd, sst, own, uown, rsb, rst, rub, rut, wt,
    ksem, vsem, s_send, s_recv, st_send, st_recv, u_send, u_recv, ut_send, ut_recv, g_send, g_recv, h_send, h_recv,
):
    me = lax.axis_index("sp")

    def device(i):
        return {"sp": i}

    def fetch(s):
        slot = s % SLOTS
        return (
            pltpu.make_async_copy(k_hbm.at[s], kb.at[slot], ksem.at[slot]),
            pltpu.make_async_copy(v_hbm.at[s], vb.at[slot], vsem.at[slot]),
        )

    def start(s):
        for copy in fetch(s):
            copy.start()

    def taken(ref, sem):
        pltpu.make_async_copy(ref, ref, sem).wait()

    def send(src, dst, send_sem, recv_sem, to):
        pltpu.make_async_remote_copy(src, dst, send_sem, recv_sem, device_id=device(to), device_id_type=pl.DeviceIdType.MESH).start()

    for s in range(SLOTS - 1):
        start(s)
    barrier = pltpu.get_barrier_semaphore()

    @pl.loop(1, N)
    def _(i):
        pl.semaphore_signal(barrier, inc=1, device_id=device(lax.rem(me + i, N)), device_id_type=pl.DeviceIdType.MESH)

    def scales(stats):
        x = stats[...].reshape(N, D)
        high = jnp.max(x, 0, keepdims=True)
        e = jnp.exp2(x - high)
        lane = lax.broadcasted_iota(jnp.int32, (N, D), 1)
        e = jnp.where(lane < H, e, 0.0)
        total = jnp.sum(pltpu.roll(x, 64, 1) * e, 0, keepdims=True)
        lane = lax.broadcasted_iota(jnp.int32, (1, D), 1)
        total = jnp.where(lane < H, total, 1.0)
        wt[...] = (e / total).T

    def together(block, mine, w):
        acc = [None] * 4
        for i in range(N):
            x = jnp.where(me == i, mine, block(i).astype(F32)) * w[:, i : i + 1]
            acc[i % 4] = x if acc[i % 4] is None else acc[i % 4] + x
        return ((acc[0] + acc[1]) + (acc[2] + acc[3])).astype(BF16)

    def give_whole():
        taken(rst.at[pl.ds(0, N - 1)], st_recv)
        taken(rsb.at[pl.ds(0, N - 1)], s_recv)
        scales(rst)
        for g in range(G):
            out[me, g] = together(lambda i: rsb[i, g], own[g], wt[8 * g : 8 * g + 8])

        @pl.loop(1, N)
        def _(i):
            send(out.at[me], out.at[me], g_send, g_recv.at[me], lax.rem(me + i, N))

    def give_unit():
        u = lax.rem(me + TAIL, N)
        s, g = WHOLE + u // G, u % G
        taken(rut.at[pl.ds(0, N - 1)], ut_recv)
        taken(rub.at[pl.ds(0, N - 1)], u_recv)
        scales(rut)
        out[s, g] = together(lambda i: rub[i], uown[...], wt[pl.ds(pl.multiple_of(8 * g, 8), 8)])

        @pl.loop(1, N)
        def _(i):
            send(out.at[s, g], out.at[s, g], h_send, h_recv, lax.rem(me + i, N))

    def work(s):
        slot = s % SLOTS
        for copy in fetch(s):
            copy.wait()
        o, m, l = attend(q_ref[s], kb.at[slot], vb.at[slot])
        row = lax.broadcasted_iota(jnp.int32, (H, D), 0)
        lane = lax.broadcasted_iota(jnp.int32, (H, D), 1)
        stats = jnp.sum(jnp.where(lane == row, m, jnp.where(lane == row + 64, l, 0.0)), 0, keepdims=True)
        sst[s] = stats
        o = o.reshape(G, 8, D)
        snd[s] = o.astype(BF16)
        return o, stats

    @pl.loop(0, WHOLE)
    def _(s):
        @pl.when(s + SLOTS - 1 < S)
        def _():
            start(s + SLOTS - 1)

        o, stats = work(s)

        @pl.when(s == 0)
        def _():
            pl.semaphore_wait(barrier, N - 1)

        @pl.when(s == me)
        def _():
            own[...] = o
            rst[me] = stats
            rsb[me] = snd[s]

        @pl.when(s != me)
        def _():
            send(sst.at[s], rst.at[me], st_send, st_recv, s)
            send(snd.at[s], rsb.at[me], s_send, s_recv, s)

        @pl.when(s == me + LAG)
        def _():
            give_whole()

    @pl.loop(WHOLE, S)
    def _(s):
        @pl.when(s + SLOTS - 1 < S)
        def _():
            start(s + SLOTS - 1)

        o, stats = work(s)
        for g in range(G):
            to = lax.rem((s - WHOLE) * G + g + N - TAIL, N)

            @pl.when(to == me)
            def _():
                uown[...] = o[g]
                rut[me] = stats
                rub[me] = snd[s, g]

            @pl.when(to != me)
            def _():
                send(sst.at[s], rut.at[me], ut_send, ut_recv, to)
                send(snd.at[s, g], rub.at[me], u_send, u_recv, to)

        @pl.when((s == me + LAG) & (me < WHOLE))
        def _():
            give_whole()

    @pl.when((me >= S - LAG) & (me < WHOLE))
    def _():
        give_whole()

    units = (me < WHOLE - TAIL) | (me >= WHOLE)

    @pl.when(units)
    def _():
        give_unit()

    @pl.loop(0, WHOLE)
    def _(s):
        @pl.when(s != me)
        def _():
            taken(out.at[s], g_recv.at[s])

    @pl.when(me < WHOLE)
    def _():
        taken(snd.at[pl.ds(0, WHOLE - 1)], s_send)
        taken(sst.at[pl.ds(0, WHOLE - 1)], st_send)
        taken(out.at[pl.ds(0, N - 1)], g_send)

    @pl.when(me >= WHOLE)
    def _():
        taken(snd.at[pl.ds(0, WHOLE)], s_send)
        taken(sst.at[pl.ds(0, WHOLE)], st_send)

    @pl.when(units)
    def _():
        taken(rub.at[pl.ds(0, UNITS - 1)], u_send)
        taken(rut.at[pl.ds(0, UNITS - 1)], ut_send)
        taken(rub.at[pl.ds(0, N - 1)], h_send)
        taken(rub.at[pl.ds(0, UNITS - 1)], h_recv)

    @pl.when(jnp.logical_not(units))
    def _():
        taken(rub.at[pl.ds(0, UNITS)], u_send)
        taken(rut.at[pl.ds(0, UNITS)], ut_send)
        taken(rub.at[pl.ds(0, UNITS)], h_recv)


def solution(mesh):
    def step(q, k, v):
        dma = pltpu.SemaphoreType.DMA
        vmem = pltpu.VMEM
        out = pl.pallas_call(
            kernel,
            out_shape=jax.ShapeDtypeStruct((S, G, 8, D), BF16),
            in_specs=[
                pl.BlockSpec(memory_space=pltpu.VMEM),
                pl.BlockSpec(memory_space=pl.ANY),
                pl.BlockSpec(memory_space=pl.ANY),
            ],
            out_specs=pl.BlockSpec(memory_space=pltpu.VMEM),
            scratch_shapes=[
                vmem((SLOTS, PAIRS, G, 16, D), BF16),
                vmem((SLOTS, PAIRS, G, 16, D), BF16),
                vmem((S, G, 8, D), BF16),
                vmem((S, 1, D), F32),
                vmem((G, 8, D), F32),
                vmem((8, D), F32),
                vmem((N, G, 8, D), BF16),
                vmem((N, 1, D), F32),
                vmem((N, 8, D), BF16),
                vmem((N, 1, D), F32),
                vmem((D, N), F32),
                dma((SLOTS,)),
                dma((SLOTS,)),
            ]
            + [dma(())] * 9 + [dma((WHOLE,))] + [dma(())] * 2,
            compiler_params=pltpu.CompilerParams(collective_id=0, has_side_effects=True, vmem_limit_bytes=60 * 2**20),
            cost_estimate=pl.CostEstimate(flops=4 * S * 128 * H * D, bytes_accessed=2 * 2 * S * 128 * H * D, transcendentals=0),
        )(q, k.reshape(S, PAIRS, G, 16, D), v.reshape(S, PAIRS, G, 16, D))
        return out.reshape(q.shape)

    return jax.shard_map(
        step,
        mesh=mesh,
        in_specs=(P("dp", None, None), P("dp", "sp", None, None), P("dp", "sp", None, None)),
        out_specs=P("dp", None, None),
        check_vma=False,
    )
```

time: 478 us -> 64.5 us (0.13)
  waiting for transfers between devices: 374 us -> 0 us
  Pallas kernels: 0 us -> 61.6 us
  matrix products: 60.9 us -> 0 us
  other arithmetic: 26.8 us -> 0 us
  between operations: 13.4 us -> 0.01 us
    all_gather x1 -> x0, waiting for transfers between devices: 374 us -> none  [step(): return together(lax.all_gather(part_of(q, k, v), 'sp')).reshape(q.shape)]
    pallas_call x0 -> x1, Pallas kernels: none -> 61.6 us  [step(): pl.pallas_call(kernel, out_shape=jax.ShapeDtypeStruct((S, G, 8, D), BF16)...]
    dot_general x2 -> x0, matrix products: 60.9 us -> none  [einsum(): return jnp.einsum(form, a.astype(jnp.float32), b.astype(jnp.float32))]
    reduce_sum x2 -> x0, other arithmetic: 22.9 us -> none  [the longest x1 21.6 us: together(): jnp.sum(seen * scale, 0) / jnp.sum(total * scale, 0)]
  transfers between devices with their start and end apart: 1 -> 0, of which waited for: 1 -> 0; matrix products, arithmetic and copies ran while one was open for 0% -> 0% of each run, Pallas kernels for 0% -> 0%
where the time goes in v1:
time: 64.5 us; the launch traced here: 63.5 us
  Pallas kernels  61.6 us (96%)
  local copies, waits for them, and re-layouts  1.82 us (3%)
    pallas_call x1, Pallas kernels, step(): pl.pallas_call(kernel, out_shape=jax.ShapeDtypeStruct((S, G, 8, D), BF16)...  61.6 us
    unnamed x1, local copies, waits for them, and re-layouts  1.82 us

profile of v1, /device:TPU:0, one launch (start us, length us, event | category | flops | bytes accessed | tf_op | source)
XLA Modules:
  0.0 63.5 jit_solution(931231037975265193)
XLA Ops:
  0.0 61.6 %shard_map.37 = bf16[32,7,8,128]{3,2,1,0:T(8,128)(2,1)} custom-call(bf16[32,56,128]{2,1,0:T(8,128)(2,1)} %q_ref.1, bf16[32,64,7,16,128]{4,3,2,1,0:T(8,128)(2,1)} %bitcast.3, bf16[32,64,7,16,128]{4,3,2,1,0:T(8,128)(2,1)} %bitcast.4), custom_call_target="tpu_custom_call" | custom-call | flops 117440512 | bytes 117440512 | tf_op jit(solution)/shard_map/pallas_call | solution.py:237
  61.6 1.8 %copy.5 = bf16[32,56,128]{2,1,0:T(8,128)(2,1)} copy(bf16[32,56,128]{2,1,0:T(8,128)(2,1)} %bitcast.5) | data formatting | bytes 917504

commit v2 on v1

--- a/solution.py
+++ b/solution.py
@@ -13,11 +13,15 @@
 D = 128
 G = 7
 PAIRS = 64
-SLOTS = 4
-TAIL = 4
-WHOLE = S - TAIL
-UNITS = TAIL * G
-LAG = 8
+SLOTS = 8
+FINE = 12
+WHOLE = S - FINE
+SIZES = (32, 32, 16, 4)
+FIRST = (0, 32, 64, 80)
+ROUNDS = len(SIZES)
+LAG = 9
+GREET = 3
+SPREAD, BACK = 5, 13
 SCALE = D**-0.5 * 1.4426950408889634
 F32 = jnp.float32
 BF16 = jnp.bfloat16
@@ -50,10 +54,25 @@
 
 
 def kernel(
-    q_ref, k_hbm, v_hbm, out, kb, vb, snd, sst, own, uown, rsb, rst, rub, rut, wt,
+    q_hbm, k_hbm, v_hbm, out, q_ref, q_sem, kb, vb, snd, sst, own, uown, rsb, rst, rub, rut, wt,
     ksem, vsem, s_send, s_recv, st_send, st_recv, u_send, u_recv, ut_send, ut_recv, g_send, g_recv, h_send, h_recv,
 ):
     me = lax.axis_index("sp")
+    mine = lax.rem(BACK * me, N)
+    turn = lax.rem(mine + N - WHOLE, N)
+    middle = lax.rem(me, 8)
+    centre = jnp.where((middle >= 2) & (middle < 6), me // 8 * 4 + middle - 2, N)
+
+    def owner(s):
+        return lax.rem(SPREAD * s, N)
+
+    def place(c):
+        return turn if c < 2 else centre
+
+    def locate(n):
+        outer = lax.rem(SPREAD * (n + WHOLE), N)
+        inner = lax.rem(n, 16) // 4 * 8 + 2 + lax.rem(n, 4)
+        return n // FIRST[1] + n // FIRST[3], outer + n // FIRST[2] * (inner - outer)
 
     def device(i):
         return {"sp": i}
@@ -75,13 +94,18 @@
     def send(src, dst, send_sem, recv_sem, to):
         pltpu.make_async_remote_copy(src, dst, send_sem, recv_sem, device_id=device(to), device_id_type=pl.DeviceIdType.MESH).start()
 
-    for s in range(SLOTS - 1):
+    start(0)
+    q_copy = pltpu.make_async_copy(q_hbm, q_ref, q_sem)
+    q_copy.start()
+    for s in range(1, SLOTS - 1):
         start(s)
     barrier = pltpu.get_barrier_semaphore()
 
     @pl.loop(1, N)
     def _(i):
         pl.semaphore_signal(barrier, inc=1, device_id=device(lax.rem(me + i, N)), device_id_type=pl.DeviceIdType.MESH)
+
+    q_copy.wait()
 
     def scales(stats):
         x = stats[...].reshape(N, D)
@@ -94,10 +118,10 @@
         total = jnp.where(lane < H, total, 1.0)
         wt[...] = (e / total).T
 
-    def together(block, mine, w):
+    def together(block, own_part, w):
         acc = [None] * 4
         for i in range(N):
-            x = jnp.where(me == i, mine, block(i).astype(F32)) * w[:, i : i + 1]
+            x = jnp.where(me == i, own_part, block(i).astype(F32)) * w[:, i : i + 1]
             acc[i % 4] = x if acc[i % 4] is None else acc[i % 4] + x
         return ((acc[0] + acc[1]) + (acc[2] + acc[3])).astype(BF16)
 
@@ -106,23 +130,29 @@
         taken(rsb.at[pl.ds(0, N - 1)], s_recv)
         scales(rst)
         for g in range(G):
-            out[me, g] = together(lambda i: rsb[i, g], own[g], wt[8 * g : 8 * g + 8])
+            out[mine, g] = together(lambda i: rsb[i, g], own[g], wt[8 * g : 8 * g + 8])
 
         @pl.loop(1, N)
         def _(i):
-            send(out.at[me], out.at[me], g_send, g_recv.at[me], lax.rem(me + i, N))
-
-    def give_unit():
-        u = lax.rem(me + TAIL, N)
-        s, g = WHOLE + u // G, u % G
-        taken(rut.at[pl.ds(0, N - 1)], ut_recv)
-        taken(rub.at[pl.ds(0, N - 1)], u_recv)
-        scales(rut)
-        out[s, g] = together(lambda i: rub[i], uown[...], wt[pl.ds(pl.multiple_of(8 * g, 8), 8)])
-
-        @pl.loop(1, N)
-        def _(i):
-            send(out.at[s, g], out.at[s, g], h_send, h_recv, lax.rem(me + i, N))
+            send(out.at[mine], out.at[mine], g_send, g_recv.at[mine], lax.rem(me + i, N))
+
+    def give_unit(c):
+        u = FIRST[c] + place(c)
+        s, g = WHOLE + u // G, lax.rem(u, G)
+        taken(rut.at[c, pl.ds(0, N - 1)], ut_recv.at[c])
+        taken(rub.at[c, pl.ds(0, N - 1)], u_recv.at[c])
+        scales(rut.at[c])
+        out[s, g] = together(lambda i: rub[c, i], uown[c], wt[pl.ds(pl.multiple_of(8 * g, 8), 8)])
+
+        for i in range(1, N):
+            send(out.at[s, g], out.at[s, g], h_send.at[c], h_recv.at[c], lax.rem(me + i, N))
+
+    def send_whole(s):
+        @pl.when(s != mine)
+        def _():
+            to = owner(s)
+            send(sst.at[s], rst.at[me], st_send, st_recv, to)
+            send(snd.at[s], rsb.at[me], s_send, s_recv, to)
 
     def work(s):
         slot = s % SLOTS
@@ -145,22 +175,23 @@
 
         o, stats = work(s)
 
-        @pl.when(s == 0)
-        def _():
-            pl.semaphore_wait(barrier, N - 1)
-
-        @pl.when(s == me)
+        @pl.when(s == mine)
         def _():
             own[...] = o
             rst[me] = stats
             rsb[me] = snd[s]
 
-        @pl.when(s != me)
-        def _():
-            send(sst.at[s], rst.at[me], st_send, st_recv, s)
-            send(snd.at[s], rsb.at[me], s_send, s_recv, s)
-
-        @pl.when(s == me + LAG)
+        @pl.when(s == GREET)
+        def _():
+            pl.semaphore_wait(barrier, N - 1)
+            for t in range(GREET):
+                send_whole(t)
+
+        @pl.when(s >= GREET)
+        def _():
+            send_whole(s)
+
+        @pl.when(s == mine + LAG)
         def _():
             give_whole()
 
@@ -172,62 +203,68 @@
 
         o, stats = work(s)
         for g in range(G):
-            to = lax.rem((s - WHOLE) * G + g + N - TAIL, N)
+            n = (s - WHOLE) * G + g
+            c, to = locate(n)
 
             @pl.when(to == me)
             def _():
-                uown[...] = o[g]
-                rut[me] = stats
-                rub[me] = snd[s, g]
+                uown[c] = o[g]
+                rut[c, me] = stats
+                rub[c, me] = snd[s, g]
 
             @pl.when(to != me)
             def _():
-                send(sst.at[s], rut.at[me], ut_send, ut_recv, to)
-                send(snd.at[s, g], rub.at[me], u_send, u_recv, to)
-
-        @pl.when((s == me + LAG) & (me < WHOLE))
+                send(sst.at[s], rut.at[c, me], ut_send.at[c], ut_recv.at[c], to)
+                send(snd.at[s, g], rub.at[c, me], u_send.at[c], u_recv.at[c], to)
+
+        @pl.when((s == mine + LAG) & (mine < WHOLE))
         def _():
             give_whole()
 
-    @pl.when((me >= S - LAG) & (me < WHOLE))
+    @pl.when((mine >= S - LAG) & (mine < WHOLE))
     def _():
         give_whole()
 
-    units = (me < WHOLE - TAIL) | (me >= WHOLE)
-
-    @pl.when(units)
-    def _():
-        give_unit()
+    for c in range(ROUNDS):
+
+        @pl.when(place(c) < SIZES[c])
+        def _(c=c):
+            give_unit(c)
 
     @pl.loop(0, WHOLE)
     def _(s):
-        @pl.when(s != me)
+        @pl.when(s != mine)
         def _():
             taken(out.at[s], g_recv.at[s])
 
-    @pl.when(me < WHOLE)
+    @pl.when(mine < WHOLE)
     def _():
         taken(snd.at[pl.ds(0, WHOLE - 1)], s_send)
         taken(sst.at[pl.ds(0, WHOLE - 1)], st_send)
         taken(out.at[pl.ds(0, N - 1)], g_send)
 
-    @pl.when(me >= WHOLE)
+    @pl.when(mine >= WHOLE)
     def _():
         taken(snd.at[pl.ds(0, WHOLE)], s_send)
         taken(sst.at[pl.ds(0, WHOLE)], st_send)
 
-    @pl.when(units)
-    def _():
-        taken(rub.at[pl.ds(0, UNITS - 1)], u_send)
-        taken(rut.at[pl.ds(0, UNITS - 1)], ut_send)
-        taken(rub.at[pl.ds(0, N - 1)], h_send)
-        taken(rub.at[pl.ds(0, UNITS - 1)], h_recv)
-
-    @pl.when(jnp.logical_not(units))
-    def _():
-        taken(rub.at[pl.ds(0, UNITS)], u_send)
-        taken(rut.at[pl.ds(0, UNITS)], ut_send)
-        taken(rub.at[pl.ds(0, UNITS)], h_recv)
+    for c in range(ROUNDS):
+
+        def settle(c, sent):
+            taken(rub.at[c, pl.ds(0, sent)], u_send.at[c])
+            taken(rut.at[c, pl.ds(0, sent)], ut_send.at[c])
+            taken(rub.at[c, pl.ds(0, sent)], h_recv.at[c])
+
+        @pl.when(place(c) < SIZES[c])
+        def _(c=c):
+            settle(c, SIZES[c] - 1)
+            taken(rub.at[c, pl.ds(0, N - 1)], h_send.at[c])
+
+        if SIZES[c] < N:
+
+            @pl.when(place(c) >= SIZES[c])
+            def _(c=c):
+                settle(c, SIZES[c])
 
 
 def solution(mesh):
@@ -238,28 +275,30 @@
             kernel,
             out_shape=jax.ShapeDtypeStruct((S, G, 8, D), BF16),
             in_specs=[
-                pl.BlockSpec(memory_space=pltpu.VMEM),
+                pl.BlockSpec(memory_space=pltpu.HBM),
                 pl.BlockSpec(memory_space=pl.ANY),
                 pl.BlockSpec(memory_space=pl.ANY),
             ],
             out_specs=pl.BlockSpec(memory_space=pltpu.VMEM),
             scratch_shapes=[
+                vmem((S, H, D), BF16),
+                dma(()),
                 vmem((SLOTS, PAIRS, G, 16, D), BF16),
                 vmem((SLOTS, PAIRS, G, 16, D), BF16),
                 vmem((S, G, 8, D), BF16),
                 vmem((S, 1, D), F32),
                 vmem((G, 8, D), F32),
-                vmem((8, D), F32),
+                vmem((ROUNDS, 8, D), F32),
                 vmem((N, G, 8, D), BF16),
                 vmem((N, 1, D), F32),
-                vmem((N, 8, D), BF16),
-                vmem((N, 1, D), F32),
+                vmem((ROUNDS, N, 8, D), BF16),
+                vmem((ROUNDS, N, 1, D), F32),
                 vmem((D, N), F32),
                 dma((SLOTS,)),
                 dma((SLOTS,)),
             ]
-            + [dma(())] * 9 + [dma((WHOLE,))] + [dma(())] * 2,
-            compiler_params=pltpu.CompilerParams(collective_id=0, has_side_effects=True, vmem_limit_bytes=60 * 2**20),
+            + [dma(())] * 4 + [dma((ROUNDS,))] * 4 + [dma(()), dma((WHOLE,))] + [dma((ROUNDS,))] * 2,
+            compiler_params=pltpu.CompilerParams(collective_id=0, has_side_effects=True, vmem_limit_bytes=40 * 2**20),
             cost_estimate=pl.CostEstimate(flops=4 * S * 128 * H * D, bytes_accessed=2 * 2 * S * 128 * H * D, transcendentals=0),
         )(q, k.reshape(S, PAIRS, G, 16, D), v.reshape(S, PAIRS, G, 16, D))
         return out.reshape(q.shape)

time: 64.5 us -> 53.8 us (0.83); the launches traced: 63.5 us -> 53.6 us
  Pallas kernels: 61.6 us -> 51.8 us
    pallas_call x1, Pallas kernels: 61.6 us -> 51.8 us  [step(): pl.pallas_call(kernel, out_shape=jax.ShapeDtypeStruct((S, G, 8, D), BF16)...]
    unnamed x1 -> x3, local copies, waits for them, and re-layouts: 1.82 us -> 1.79 us
where the time goes in v2:
time: 53.8 us; the launch traced here: 53.6 us
  Pallas kernels  51.8 us (96%)
  local copies, waits for them, and re-layouts  1.79 us (3%)
    pallas_call x1, Pallas kernels, step(): pl.pallas_call(kernel, out_shape=jax.ShapeDtypeStruct((S, G, 8, D), BF16)...  51.8 us
    unnamed x3, local copies, waits for them, and re-layouts  1.79 us

profile of v2, /device:TPU:0, one launch (start us, length us, event | category | flops | bytes accessed | tf_op | source)
XLA Modules:
  0.0 53.6 jit_solution(2795167272123913219)
XLA Ops:
  0.0 0.0 copy-start
  0.0 1.0 %copy-done = bf16[32,56,128]{2,1,0:T(8,128)(2,1)S(1)} copy-done((bf16[32,56,128]{2,1,0:T(8,128)(2,1)S(1)}, bf16[32,56,128]{2,1,0:T(8,128)(2,1)}, u32[]{:S(2)}) %copy-start) | copy-done | bytes 458776
  1.0 51.8 %shard_map.37 = bf16[32,7,8,128]{3,2,1,0:T(8,128)(2,1)S(1)} custom-call(bf16[32,56,128]{2,1,0:T(8,128)(2,1)S(1)} %copy-done, bf16[32,64,7,16,128]{4,3,2,1,0:T(8,128)(2,1)} %bitcast.4, bf16[32,64,7,16,128]{4,3,2,1,0:T(8,128)(2,1)} %bitcast.5), custom_call_target="tpu_custom_call" | custom-call | flops 117440512 | bytes 117440512 | tf_op jit(solution)/shard_map/pallas_call | solution.py:274
  52.9 0.8 %copy.5 = bf16[32,56,128]{2,1,0:T(8,128)(2,1)} copy(bf16[32,56,128]{2,1,0:T(8,128)(2,1)S(1)} %bitcast.3) | data formatting | bytes 917504
Async XLA Ops:
  0.0 1.0 %copy-start = (bf16[32,56,128]{2,1,0:T(8,128)(2,1)S(1)}, bf16[32,56,128]{2,1,0:T(8,128)(2,1)}, u32[]{:S(2)}) copy-start(bf16[32,56,128]{2,1,0:T(8,128)(2,1)} %q_hbm.1) | copy-start | bytes 1376260

commit v3 on v2

--- a/solution.py
+++ b/solution.py
@@ -14,12 +14,14 @@
 G = 7
 PAIRS = 64
 SLOTS = 8
+GRANT = 55888896
 FINE = 12
 WHOLE = S - FINE
-SIZES = (32, 32, 16, 4)
-FIRST = (0, 32, 64, 80)
-ROUNDS = len(SIZES)
-LAG = 9
+COUNTS = (4, 4, 2, 2)
+BEGINS = (20, 24, 28, 30)
+ROUNDS = len(COUNTS)
+SIZES = tuple(G * n for n in COUNTS)
+LAG = 8
 GREET = 3
 SPREAD, BACK = 5, 13
 SCALE = D**-0.5 * 1.4426950408889634
@@ -28,29 +30,27 @@
 
 
 def attend(q, kbuf, vbuf):
-    qf = q.astype(F32)
+    qf = q.astype(F32).reshape(H, D)
     q2 = jnp.concatenate([qf, qf], 0).astype(BF16)
     col = lax.broadcasted_iota(jnp.int32, (16, 16 * PAIRS), 1)
     row = lax.broadcasted_iota(jnp.int32, (16, 16 * PAIRS), 0)
     mask = (col & 15) == row
-    s, m = [], []
+    x = [
+        lax.dot_general(q2[16 * g : 16 * g + 16], kbuf[:, g].reshape(16 * PAIRS, D), (((1,), (1,)), ((), ())), preferred_element_type=F32)
+        for g in range(G)
+    ]
+    e, m, l = [], [], []
     for g in range(G):
-        kg = kbuf[:, g].reshape(16 * PAIRS, D)
-        x = lax.dot_general(q2[16 * g : 16 * g + 16], kg, (((1,), (1,)), ((), ())), preferred_element_type=F32)
-        x = jnp.where(mask, x * SCALE, -jnp.inf)
-        s.append(x)
-        m.append(jnp.max(x, 1, keepdims=True))
-    m = jnp.concatenate(m, 0)
+        y = jnp.where(mask, x[g] * SCALE, -jnp.inf)
+        m.append(jnp.max(y, 1, keepdims=True))
+        y = jnp.exp2(y - m[g])
+        l.append(jnp.sum(y, 1, keepdims=True))
+        e.append(y.astype(BF16))
+    o = [jnp.dot(e[g], vbuf[:, g].reshape(16 * PAIRS, D), preferred_element_type=F32) for g in range(G)]
+    o, m, l = (jnp.concatenate(part, 0) for part in (o, m, l))
     high = jnp.maximum(m[:H], m[H:])
-    both = jnp.concatenate([high, high], 0)
-    o, l = [], []
-    for g in range(G):
-        e = jnp.exp2(s[g] - both[16 * g : 16 * g + 16])
-        l.append(jnp.sum(e, 1, keepdims=True))
-        o.append(jnp.dot(e.astype(BF16), vbuf[:, g].reshape(16 * PAIRS, D), preferred_element_type=F32))
-    l = jnp.concatenate(l, 0)
-    o = jnp.concatenate(o, 0)
-    return o[:H] + o[H:], high, l[:H] + l[H:]
+    even, odd = jnp.exp2(m[:H] - high), jnp.exp2(m[H:] - high)
+    return o[:H] * even + o[H:] * odd, high, l[:H] * even + l[H:] * odd
 
 
 def kernel(
@@ -69,10 +69,10 @@
     def place(c):
         return turn if c < 2 else centre
 
-    def locate(n):
-        outer = lax.rem(SPREAD * (n + WHOLE), N)
-        inner = lax.rem(n, 16) // 4 * 8 + 2 + lax.rem(n, 4)
-        return n // FIRST[1] + n // FIRST[3], outer + n // FIRST[2] * (inner - outer)
+    def unit_owner(c, u):
+        if c < 2:
+            return lax.rem(SPREAD * u + SPREAD * WHOLE, N)
+        return u + 2 + u // 4 * 4
 
     def device(i):
         return {"sp": i}
@@ -94,11 +94,9 @@
     def send(src, dst, send_sem, recv_sem, to):
         pltpu.make_async_remote_copy(src, dst, send_sem, recv_sem, device_id=device(to), device_id_type=pl.DeviceIdType.MESH).start()
 
-    start(0)
     q_copy = pltpu.make_async_copy(q_hbm, q_ref, q_sem)
     q_copy.start()
-    for s in range(1, SLOTS - 1):
-        start(s)
+    start(0)
     barrier = pltpu.get_barrier_semaphore()
 
     @pl.loop(1, N)
@@ -106,6 +104,8 @@
         pl.semaphore_signal(barrier, inc=1, device_id=device(lax.rem(me + i, N)), device_id_type=pl.DeviceIdType.MESH)
 
     q_copy.wait()
+    for s in range(1, SLOTS - 1):
+        start(s)
 
     def scales(stats):
         x = stats[...].reshape(N, D)
@@ -137,8 +137,7 @@
             send(out.at[mine], out.at[mine], g_send, g_recv.at[mine], lax.rem(me + i, N))
 
     def give_unit(c):
-        u = FIRST[c] + place(c)
-        s, g = WHOLE + u // G, lax.rem(u, G)
+        s, g = BEGINS[c] + place(c) // G, lax.rem(place(c), G)
         taken(rut.at[c, pl.ds(0, N - 1)], ut_recv.at[c])
         taken(rub.at[c, pl.ds(0, N - 1)], u_recv.at[c])
         scales(rut.at[c])
@@ -195,35 +194,34 @@
         def _():
             give_whole()
 
-    @pl.loop(WHOLE, S)
-    def _(s):
-        @pl.when(s + SLOTS - 1 < S)
-        def _():
-            start(s + SLOTS - 1)
-
-        o, stats = work(s)
-        for g in range(G):
-            n = (s - WHOLE) * G + g
-            c, to = locate(n)
-
-            @pl.when(to == me)
+    for c in range(ROUNDS):
+
+        @pl.loop(BEGINS[c], BEGINS[c] + COUNTS[c])
+        def _(s, c=c):
+            @pl.when(s + SLOTS - 1 < S)
             def _():
-                uown[c] = o[g]
-                rut[c, me] = stats
-                rub[c, me] = snd[s, g]
-
-            @pl.when(to != me)
-            def _():
-                send(sst.at[s], rut.at[c, me], ut_send.at[c], ut_recv.at[c], to)
-                send(snd.at[s, g], rub.at[c, me], u_send.at[c], u_recv.at[c], to)
-
-        @pl.when((s == mine + LAG) & (mine < WHOLE))
-        def _():
-            give_whole()
-
-    @pl.when((mine >= S - LAG) & (mine < WHOLE))
-    def _():
-        give_whole()
+                start(s + SLOTS - 1)
+
+            o, stats = work(s)
+            for g in range(G):
+                to = unit_owner(c, (s - BEGINS[c]) * G + g)
+
+                @pl.when(to == me)
+                def _(g=g):
+                    uown[c] = o[g]
+                    rut[c, me] = stats
+                    rub[c, me] = snd[s, g]
+
+                @pl.when(to != me)
+                def _(g=g, to=to):
+                    send(snd.at[s, g], rub.at[c, me], u_send.at[c], u_recv.at[c], to)
+                    send(sst.at[s], rut.at[c, me], ut_send.at[c], ut_recv.at[c], to)
+
+            if BEGINS[c] < WHOLE + LAG:
+
+                @pl.when((s == mine + LAG) & (mine < WHOLE))
+                def _():
+                    give_whole()
 
     for c in range(ROUNDS):
 
@@ -275,13 +273,13 @@
             kernel,
             out_shape=jax.ShapeDtypeStruct((S, G, 8, D), BF16),
             in_specs=[
-                pl.BlockSpec(memory_space=pltpu.HBM),
+                pl.BlockSpec(memory_space=pl.ANY),
                 pl.BlockSpec(memory_space=pl.ANY),
                 pl.BlockSpec(memory_space=pl.ANY),
             ],
             out_specs=pl.BlockSpec(memory_space=pltpu.VMEM),
             scratch_shapes=[
-                vmem((S, H, D), BF16),
+                vmem((S, G, 8, D), BF16),
                 dma(()),
                 vmem((SLOTS, PAIRS, G, 16, D), BF16),
                 vmem((SLOTS, PAIRS, G, 16, D), BF16),
@@ -298,9 +296,9 @@
                 dma((SLOTS,)),
             ]
             + [dma(())] * 4 + [dma((ROUNDS,))] * 4 + [dma(()), dma((WHOLE,))] + [dma((ROUNDS,))] * 2,
-            compiler_params=pltpu.CompilerParams(collective_id=0, has_side_effects=True, vmem_limit_bytes=40 * 2**20),
+            compiler_params=pltpu.CompilerParams(collective_id=0, has_side_effects=True, vmem_limit_bytes=GRANT),
             cost_estimate=pl.CostEstimate(flops=4 * S * 128 * H * D, bytes_accessed=2 * 2 * S * 128 * H * D, transcendentals=0),
-        )(q, k.reshape(S, PAIRS, G, 16, D), v.reshape(S, PAIRS, G, 16, D))
+        )(q.reshape(S, G, 8, D), k.reshape(S, PAIRS, G, 16, D), v.reshape(S, PAIRS, G, 16, D))
         return out.reshape(q.shape)
 
     return jax.shard_map(

time: 53.8 us -> 51.2 us (0.952)
  Pallas kernels: 51.8 us -> 50.2 us
  local copies, waits for them, and re-layouts: 1.79 us -> 0.77 us
    pallas_call x1, Pallas kernels: 51.8 us -> 50.2 us  [step(): pl.pallas_call(kernel, out_shape=jax.ShapeDtypeStruct((S, G, 8, D), BF16)...]
    unnamed x3 -> x1, local copies, waits for them, and re-layouts: 1.79 us -> 0.77 us
where the time goes in v3:
time: 51.2 us; the launch traced here: 51 us
  Pallas kernels  50.2 us (98%)
  local copies, waits for them, and re-layouts  0.77 us (2%)
    pallas_call x1, Pallas kernels, step(): pl.pallas_call(kernel, out_shape=jax.ShapeDtypeStruct((S, G, 8, D), BF16)...  50.2 us

profile of v3, /device:TPU:0, one launch (start us, length us, event | category | flops | bytes accessed | tf_op | source)
XLA Modules:
  0.0 51.0 jit_solution(8604815932371883746)
XLA Ops:
  0.0 50.2 %shard_map.37 = bf16[32,7,8,128]{3,2,1,0:T(8,128)(2,1)S(1)} custom-call(bf16[32,7,8,128]{3,2,1,0:T(8,128)(2,1)} %bitcast.7, bf16[32,64,7,16,128]{4,3,2,1,0:T(8,128)(2,1)} %bitcast.5, bf16[32,64,7,16,128]{4,3,2,1,0:T(8,128)(2,1)} %bitcast.6), custom_call_target="tpu_custom_call" | custom-call | flops 117440512 | bytes 117440512 | tf_op jit(solution)/shard_map/pallas_call | solution.py:272
  50.3 0.8 %copy.5 = bf16[32,56,128]{2,1,0:T(8,128)(2,1)} copy(bf16[32,56,128]{2,1,0:T(8,128)(2,1)S(1)} %bitcast.4) | data formatting | bytes 917504
